TPU v7x, 128 devices: a whole 4x4x4 slice. The times are simulated.
128 devices in a mesh: atom: 32 (over y, z, core), aux: 4 (over x).
Axes of the slice: x: 4, y: 4, z: 4, core: 2. Of those that a mesh axis runs over, the one named last changes fastest.
Arguments:
- pao_blocks: bfloat16 [64, 24, 15360], P('atom', None, 'aux'), may hold values from -0.048339844 to 0.048339844
- cabs_blocks: bfloat16 [64, 48, 15360], P('atom', None, 'aux'), may hold values from -0.3046875 to 0.3046875
- cabs_weight: bfloat16 [64, 48], P('atom'), may hold values from 0.25 to 4
- pair_blocks: int32 [2048, 4], P('atom'), may hold values from 0 to 63, as said below
- pao_size: int32 [2048], P('atom'), may hold values from 24 to 96
- cabs_size: int32 [2048], P('atom'), may hold values from 48 to 192
Outputs:
- v_pairs: float32 [2048, 96, 96], P('atom', 'aux')
Inputs may be any that keep to these rules, and one draw needn't show every extreme that they name: `pair_blocks`: each row names 4 different atom blocks; atom block b belongs to owner b // 2, and the 64 rows of one index of atom name at most one block of each owner.
All inputs are finite; a program needn't handle non-finite values.
Results may differ from a plain program's by a relative error of at most 0.0003.
Values may be sent and summed in bfloat16 or wider, within the bound.
A program may use at most 128 MiB of HBM per device.

v0:
```python
import jax
import jax.numpy as jnp
from jax import lax
from jax.sharding import PartitionSpec as P


def sent_together(arrays, axis, dim, along):
    ends, at = ([], 0)
    for a in arrays[:-1]:
        at += a.shape[along]
        ends.append(at)
    both = jnp.concatenate(arrays, axis=along)
    return tuple(
        jnp.split(lax.psum_scatter(both, axis, scatter_dimension=dim, tiled=True), ends, axis=along)
    )


def collect(pieces):
    return (pieces[0], pieces[1], pieces[2])


def shards(pao_blocks, cabs_blocks, cabs_weight, pair_blocks, pao_size, cabs_size):
    owners = lax.axis_size("atom")
    blk_dev = pao_blocks.shape[0]
    pao_rows = pao_blocks.shape[1]
    cabs_rows = cabs_blocks.shape[1]
    aux_local = pao_blocks.shape[2]
    pair_count = pair_blocks.shape[0]
    dom_count = pair_blocks.shape[1]
    pao_width = dom_count * pao_rows
    cabs_width = dom_count * cabs_rows
    flat_blocks = pair_blocks.reshape(-1)
    owner_ids = flat_blocks // blk_dev
    owner_range = jnp.arange(owners, dtype=jnp.int32)
    matches = owner_ids[:, None] == owner_range[None, :]
    wanted = jnp.max(jnp.where(matches, flat_blocks[:, None], -1), axis=0)
    every_pao, every_cabs, every_weight = collect(
        (
            lax.all_gather(pao_blocks, "atom", axis=0, tiled=True),
            lax.all_gather(cabs_blocks, "atom", axis=0, tiled=True),
            lax.all_gather(cabs_weight, "atom", axis=0, tiled=True),
        )
    )
    chosen = jnp.maximum(wanted, 0)
    slot_pao = jnp.take(every_pao, chosen, axis=0)
    slot_cabs = jnp.take(every_cabs, chosen, axis=0)
    slot_weight = jnp.take(every_weight, chosen, axis=0)
    slot_of = owner_ids.reshape(pair_count, dom_count)
    group_size = 4
    groups = slot_of.reshape(pair_count // group_size, group_size, dom_count)

    def pair_products(slots):
        rows_pao = jnp.take(slot_pao, slots.reshape(-1), axis=0).reshape(
            group_size, pao_width, aux_local
        )
        rows_cabs = jnp.take(slot_cabs, slots.reshape(-1), axis=0).reshape(
            group_size, cabs_width, aux_local
        )
        margin_part = jnp.einsum(
            "pia,pja->pij", rows_pao, rows_pao, preferred_element_type=jnp.float32
        )
        coupling_part = jnp.einsum(
            "pia,pja->pij", rows_pao, rows_cabs, preferred_element_type=jnp.float32
        )
        return (margin_part, coupling_part)

    margin, coupling = lax.map(pair_products, groups)
    margin = margin.reshape(pair_count, pao_width, pao_width)
    coupling = coupling.reshape(pair_count, pao_width, cabs_width)
    keep_pao = (jnp.arange(pao_width, dtype=jnp.int32)[None, :] < pao_size[:, None]).astype(
        jnp.float32
    )
    keep_cabs = (jnp.arange(cabs_width, dtype=jnp.int32)[None, :] < cabs_size[:, None]).astype(
        jnp.float32
    )
    margin = margin * keep_pao[:, :, None] * keep_pao[:, None, :]
    coupling = coupling * keep_pao[:, :, None] * keep_cabs[:, None, :]
    scales = (
        jnp.take(slot_weight, slot_of.reshape(-1), axis=0)
        .reshape(pair_count, cabs_width)
        .astype(jnp.float32)
    )
    margin_rows, coupling_rows = sent_together((margin, coupling), "aux", 1, 2)
    coupling_full = lax.all_gather(coupling_rows, "aux", axis=1, tiled=True)
    return margin_rows - jnp.einsum(
        "pix,pjx->pij",
        coupling_rows * scales[:, None, :],
        coupling_full,
        precision=lax.Precision.HIGHEST,
    )


def solution(mesh):
    placed = (
        P("atom", None, "aux"),
        P("atom", None, "aux"),
        P("atom", None),
        P("atom", None),
        P("atom"),
        P("atom"),
    )
    return jax.shard_map(
        shards, mesh=mesh, in_specs=placed, out_specs=P("atom", "aux", None), check_vma=False
    )
```

profile of v0, /device:TPU:1, one launch (start us, length us, event | category | flops | bytes accessed | tf_op | source)
XLA Modules:
  0.0 740.0 jit_solution(4457633753350145893)
XLA Ops:
  10.6 63.6 %all-gather.5.cloned.1.call-done = bf16[64,24,3840]{2,1,0:T(8,128)(2,1)} async-done(((bf16[2,24,3840]{2,1,0:T(8,128)(2,1)}), bf16[64,24,3840]{2,1,0:T(8,128)(2,1)}) %all-gather.5.cloned.1.call-update) | async-done | bytes 11796496 | tf_op jit(solution)/shard_map/all_gather | solution.py:39
  74.3 7.9 %gather_fusion.2 = bf16[32,24,3840]{2,1,0:T(8,128)(2,1)} fusion(bf16[64,24,3840]{2,1,0:T(8,128)(2,1)} %all-gather.5.cloned.1.call-done, s32[1024]{0:T(1024)S(1)} %pad_clamp_fusion.2), kind=kCustom, calls=%fused_computation.2 | custom fusion | bytes 11796608 | tf_op jit(solution)/shard_map/jit(_take)/gather | solution.py:45
  82.1 5.9 broadcast_select_fusion.1
  88.0 76.2 %all-gather.7.cloned.1.call-done = bf16[64,48,3840]{2,1,0:T(8,128)(2,1)} async-done(((bf16[2,48,3840]{2,1,0:T(8,128)(2,1)}), bf16[64,48,3840]{2,1,0:T(8,128)(2,1)}) %all-gather.7.cloned.1.call-update) | async-done | bytes 23592976 | tf_op jit(solution)/shard_map/all_gather | solution.py:40
  164.2 14.1 %gather_fusion.3 = bf16[32,48,3840]{2,1,0:T(8,128)(2,1)} fusion(bf16[64,48,3840]{2,1,0:T(8,128)(2,1)} %all-gather.7.cloned.1.call-done, s32[1024]{0:T(1024)S(1)} %pad_clamp_fusion.2), kind=kCustom, calls=%fused_computation.3 | custom fusion | bytes 23593088 | tf_op jit(solution)/shard_map/jit(_take)/gather | solution.py:46
  178.4 10.3 %broadcast_select_fusion = bf16[32,48,3840]{2,1,0:T(8,128)(2,1)} fusion(bf16[32,48,3840]{2,1,0:T(8,128)(2,1)} %gather_fusion.3, pred[32]{0:T(512)(128)(4,1)S(1)} %broadcast_compare_fusion), kind=kLoop, calls=%fused_computation.18 | loop fusion | flops 5898240 | bytes 23592992 | tf_op jit(solution)/shard_map/jit(_take)/select_n | solution.py:46
  188.6 368.7 %while.12 = (s32[]{:T(128)}, f32[16,4,96,96]{3,2,1,0:T(8,128)}, f32[16,4,96,192]{3,2,1,0:T(8,128)}, s32[16,4,4]{2,1,0:T(4,128)S(1)}, bf16[32,24,3840]{2,1,0:T(8,...) while((s32[]{:T(128)}, f32[16,4,96,96]{3,2,1,0:T(8,128)}, f32[16,4,96,192]{3,2,1,0:T(8,128)}, ...), condition=%wide.region_2.3_spmd, body=%wide.region_1.2_spmd.sunk | while | flops 853771392 | bytes 50735296 | solution.py:67
  188.8 5.0 gather_fusion
  196.1 7.8 %gather_fusion.1 = bf16[16,48,3840]{2,1,0:T(8,128)(2,1)} fusion(bf16[32,48,3840]{2,1,0:T(8,128)(2,1)} %get-tuple-element.114, s32[1024]{0:T(1024)S(1)} %pad_clamp_fusion.4), kind=kCustom, calls=%fused_computation.1.clone.1 | custom fusion | bytes 11796544 | tf_op jit(solution)/shard_map/while/body/eval_jaxpr/jit(_take)/gather | solution.py:56
  204.1 3.3 bitcast_select_fusion.5
  211.8 5.0 gather_fusion
  219.1 7.8 %gather_fusion.1 = bf16[16,48,3840]{2,1,0:T(8,128)(2,1)} fusion(bf16[32,48,3840]{2,1,0:T(8,128)(2,1)} %get-tuple-element.114, s32[1024]{0:T(1024)S(1)} %pad_clamp_fusion.4), kind=kCustom, calls=%fused_computation.1.clone.1 | custom fusion | bytes 11796544 | tf_op jit(solution)/shard_map/while/body/eval_jaxpr/jit(_take)/gather | solution.py:56
  227.1 3.3 bitcast_select_fusion.5
  230.4 2.8 fusion.36
  234.9 5.0 gather_fusion
  242.2 7.8 %gather_fusion.1 = bf16[16,48,3840]{2,1,0:T(8,128)(2,1)} fusion(bf16[32,48,3840]{2,1,0:T(8,128)(2,1)} %get-tuple-element.114, s32[1024]{0:T(1024)S(1)} %pad_clamp_fusion.4), kind=kCustom, calls=%fused_computation.1.clone.1 | custom fusion | bytes 11796544 | tf_op jit(solution)/shard_map/while/body/eval_jaxpr/jit(_take)/gather | solution.py:56
  250.2 3.3 bitcast_select_fusion.5
  257.9 5.0 gather_fusion
  265.3 7.8 %gather_fusion.1 = bf16[16,48,3840]{2,1,0:T(8,128)(2,1)} fusion(bf16[32,48,3840]{2,1,0:T(8,128)(2,1)} %get-tuple-element.114, s32[1024]{0:T(1024)S(1)} %pad_clamp_fusion.4), kind=kCustom, calls=%fused_computation.1.clone.1 | custom fusion | bytes 11796544 | tf_op jit(solution)/shard_map/while/body/eval_jaxpr/jit(_take)/gather | solution.py:56
  273.2 3.3 bitcast_select_fusion.5
  280.9 5.0 gather_fusion
  288.3 7.8 %gather_fusion.1 = bf16[16,48,3840]{2,1,0:T(8,128)(2,1)} fusion(bf16[32,48,3840]{2,1,0:T(8,128)(2,1)} %get-tuple-element.114, s32[1024]{0:T(1024)S(1)} %pad_clamp_fusion.4), kind=kCustom, calls=%fused_computation.1.clone.1 | custom fusion | bytes 11796544 | tf_op jit(solution)/shard_map/while/body/eval_jaxpr/jit(_take)/gather | solution.py:56
  296.3 3.3 bitcast_select_fusion.5
  299.5 2.8 fusion.36
  304.0 5.0 gather_fusion
  311.3 7.8 %gather_fusion.1 = bf16[16,48,3840]{2,1,0:T(8,128)(2,1)} fusion(bf16[32,48,3840]{2,1,0:T(8,128)(2,1)} %get-tuple-element.114, s32[1024]{0:T(1024)S(1)} %pad_clamp_fusion.4), kind=kCustom, calls=%fused_computation.1.clone.1 | custom fusion | bytes 11796544 | tf_op jit(solution)/shard_map/while/body/eval_jaxpr/jit(_take)/gather | solution.py:56
  319.3 3.3 bitcast_select_fusion.5
  327.0 5.0 gather_fusion
  334.4 7.8 %gather_fusion.1 = bf16[16,48,3840]{2,1,0:T(8,128)(2,1)} fusion(bf16[32,48,3840]{2,1,0:T(8,128)(2,1)} %get-tuple-element.114, s32[1024]{0:T(1024)S(1)} %pad_clamp_fusion.4), kind=kCustom, calls=%fused_computation.1.clone.1 | custom fusion | bytes 11796544 | tf_op jit(solution)/shard_map/while/body/eval_jaxpr/jit(_take)/gather | solution.py:56
  342.4 3.3 bitcast_select_fusion.5
  350.1 5.0 gather_fusion
  357.4 7.8 %gather_fusion.1 = bf16[16,48,3840]{2,1,0:T(8,128)(2,1)} fusion(bf16[32,48,3840]{2,1,0:T(8,128)(2,1)} %get-tuple-element.114, s32[1024]{0:T(1024)S(1)} %pad_clamp_fusion.4), kind=kCustom, calls=%fused_computation.1.clone.1 | custom fusion | bytes 11796544 | tf_op jit(solution)/shard_map/while/body/eval_jaxpr/jit(_take)/gather | solution.py:56
  365.4 3.3 bitcast_select_fusion.5
  373.2 5.0 gather_fusion
  380.5 7.8 %gather_fusion.1 = bf16[16,48,3840]{2,1,0:T(8,128)(2,1)} fusion(bf16[32,48,3840]{2,1,0:T(8,128)(2,1)} %get-tuple-element.114, s32[1024]{0:T(1024)S(1)} %pad_clamp_fusion.4), kind=kCustom, calls=%fused_computation.1.clone.1 | custom fusion | bytes 11796544 | tf_op jit(solution)/shard_map/while/body/eval_jaxpr/jit(_take)/gather | solution.py:56
  388.5 3.3 bitcast_select_fusion.5
  396.2 5.0 gather_fusion
  403.5 7.8 %gather_fusion.1 = bf16[16,48,3840]{2,1,0:T(8,128)(2,1)} fusion(bf16[32,48,3840]{2,1,0:T(8,128)(2,1)} %get-tuple-element.114, s32[1024]{0:T(1024)S(1)} %pad_clamp_fusion.4), kind=kCustom, calls=%fused_computation.1.clone.1 | custom fusion | bytes 11796544 | tf_op jit(solution)/shard_map/while/body/eval_jaxpr/jit(_take)/gather | solution.py:56
  411.5 3.3 bitcast_select_fusion.5
  419.2 5.0 gather_fusion
  426.6 7.8 %gather_fusion.1 = bf16[16,48,3840]{2,1,0:T(8,128)(2,1)} fusion(bf16[32,48,3840]{2,1,0:T(8,128)(2,1)} %get-tuple-element.114, s32[1024]{0:T(1024)S(1)} %pad_clamp_fusion.4), kind=kCustom, calls=%fused_computation.1.clone.1 | custom fusion | bytes 11796544 | tf_op jit(solution)/shard_map/while/body/eval_jaxpr/jit(_take)/gather | solution.py:56
  434.6 3.3 bitcast_select_fusion.5
  442.3 5.0 gather_fusion
  449.6 7.8 %gather_fusion.1 = bf16[16,48,3840]{2,1,0:T(8,128)(2,1)} fusion(bf16[32,48,3840]{2,1,0:T(8,128)(2,1)} %get-tuple-element.114, s32[1024]{0:T(1024)S(1)} %pad_clamp_fusion.4), kind=kCustom, calls=%fused_computation.1.clone.1 | custom fusion | bytes 11796544 | tf_op jit(solution)/shard_map/while/body/eval_jaxpr/jit(_take)/gather | solution.py:56
  457.6 3.3 bitcast_select_fusion.5
  460.9 2.8 fusion.36
  465.3 5.0 gather_fusion
  472.6 7.8 %gather_fusion.1 = bf16[16,48,3840]{2,1,0:T(8,128)(2,1)} fusion(bf16[32,48,3840]{2,1,0:T(8,128)(2,1)} %get-tuple-element.114, s32[1024]{0:T(1024)S(1)} %pad_clamp_fusion.4), kind=kCustom, calls=%fused_computation.1.clone.1 | custom fusion | bytes 11796544 | tf_op jit(solution)/shard_map/while/body/eval_jaxpr/jit(_take)/gather | solution.py:56
  480.6 3.3 bitcast_select_fusion.5
  488.4 5.0 gather_fusion
  495.7 7.8 %gather_fusion.1 = bf16[16,48,3840]{2,1,0:T(8,128)(2,1)} fusion(bf16[32,48,3840]{2,1,0:T(8,128)(2,1)} %get-tuple-element.114, s32[1024]{0:T(1024)S(1)} %pad_clamp_fusion.4), kind=kCustom, calls=%fused_computation.1.clone.1 | custom fusion | bytes 11796544 | tf_op jit(solution)/shard_map/while/body/eval_jaxpr/jit(_take)/gather | solution.py:56
  503.7 3.3 bitcast_select_fusion.5
  511.4 5.0 gather_fusion
  518.7 7.8 %gather_fusion.1 = bf16[16,48,3840]{2,1,0:T(8,128)(2,1)} fusion(bf16[32,48,3840]{2,1,0:T(8,128)(2,1)} %get-tuple-element.114, s32[1024]{0:T(1024)S(1)} %pad_clamp_fusion.4), kind=kCustom, calls=%fused_computation.1.clone.1 | custom fusion | bytes 11796544 | tf_op jit(solution)/shard_map/while/body/eval_jaxpr/jit(_take)/gather | solution.py:56
  526.7 3.3 bitcast_select_fusion.5
  534.4 5.0 gather_fusion
  541.8 7.8 %gather_fusion.1 = bf16[16,48,3840]{2,1,0:T(8,128)(2,1)} fusion(bf16[32,48,3840]{2,1,0:T(8,128)(2,1)} %get-tuple-element.114, s32[1024]{0:T(1024)S(1)} %pad_clamp_fusion.4), kind=kCustom, calls=%fused_computation.1.clone.1 | custom fusion | bytes 11796544 | tf_op jit(solution)/shard_map/while/body/eval_jaxpr/jit(_take)/gather | solution.py:56
  549.7 3.3 bitcast_select_fusion.5
  562.5 6.1 pad_maximum_fusion
  568.7 87.8 %reduce-scatter.2.cloned.1.call-done = f32[64,24,288]{2,1,0:T(8,128)} async-done(((f32[64,96,288]{2,1,0:T(8,128)}), f32[64,24,288]{2,1,0:T(8,128)}) %reduce-scatter.2.cloned.1.call-update) | async-done | bytes 1769488 | tf_op jit(solution)/shard_map/reduce_scatter | solution.py:14
  656.6 3.4 split.9
  660.1 22.5 %all-gather = bf16[32,2,48]{2,1,0:T(2,128)(2,1)S(1)} all-gather(bf16[1,2,48]{2,1,0:T(2,128)(2,1)S(1)} %bitcast.64), channel_id=1, replica_groups=mesh['atom'=32,'aux'=4] {'atom'}, dimensions={0}, use_global_device_ids=true | all-gather | bytes 6336 | tf_op jit(solution)/shard_map/all_gather | solution.py:41
  684.5 41.0 %all-gather.9.cloned.1.call-done = f32[64,96,192]{2,1,0:T(8,128)} async-done(((f32[64,24,192]{2,1,0:T(8,128)}), f32[64,96,192]{2,1,0:T(8,128)}) %all-gather.9.cloned.1.call-update) | async-done | bytes 4718608 | tf_op jit(solution)/shard_map/all_gather | solution.py:84
  725.4 8.0 %fusion.7 = f32[64,24,96]{2,1,0:T(8,128)} fusion(f32[64,96,192]{2,1,0:T(8,128)} %all-gather.9.cloned.1.call-done, f32[64,24,288]{2,1,0:T(8,128)S(1)} %copy-done.1, f32[64,192]{1,0:T(8,128)S(1)} %select_convert_fusion), kind=kOutput, calls=%fused_computation.27 | convolution fusion | flops 340180992 | bytes 7127040 | tf_op jit(solution)/shard_map/pix,pjx->pij/dot_general | solution.py:85
  (214 shorter events, 113.7 us)
Async XLA Ops:
  6.5 67.7 %all-gather.5.cloned.1.call-start = ((), (), s32[]{:S(2)}) async-start(), calls=%async_computation.1 | async-start | bytes 12165120 | tf_op jit(solution)/shard_map/all_gather | solution.py:39
  7.3 157.0 %all-gather.7.cloned.1.call-start = ((), (), s32[]{:S(2)}) async-start(), calls=%async_computation.2 | async-start | bytes 24330240 | tf_op jit(solution)/shard_map/all_gather | solution.py:40
  8.0 648.6 %reduce-scatter.2.cloned.1.call-start = ((), (), s32[]{:S(2)}) async-start(), calls=%async_computation.3 | async-start | bytes 11796480 | tf_op jit(solution)/shard_map/reduce_scatter | solution.py:14
  557.3 3.7 copy-start
  568.6 91.5 %copy-start.3 = (bf16[2,48]{1,0:T(2,128)(2,1)S(1)}, bf16[2,48]{1,0:T(2,128)(2,1)}, u32[]{:S(2)}) copy-start(bf16[2,48]{1,0:T(2,128)(2,1)} %param.10) | copy-start | bytes 580
  568.7 115.7 %copy-start.2 = (s32[64,4]{0,1:T(4,128)S(1)}, s32[64,4]{0,1:T(4,128)}, u32[]{:S(2)}) copy-start(s32[64,4]{0,1:T(4,128)} %param.11) | copy-start | bytes 3076
  568.7 156.8 %all-gather.9.cloned.1.call-start = ((), (), s32[]{:S(2)}) async-start(), calls=%async_computation.4 | async-start | bytes 7864320 | tf_op jit(solution)/shard_map/all_gather | solution.py:84
  656.6 68.9 %copy-start.1 = (f32[64,24,288]{2,1,0:T(8,128)S(1)}, f32[64,24,288]{2,1,0:T(8,128)}, u32[]{:S(2)}) copy-start(f32[64,24,288]{2,1,0:T(8,128)} %reduce-scatter.2.cloned.1.call-done) | copy-start | bytes 5308420
Sparse Core Ops, SparseCore 0:
  9.6 64.6 all-gather.4
  76.5 87.6 all-gather.6
  568.8 87.7 reduce-scatter.1
  660.1 65.2 all-gather.8
where the time goes:
time: 743 us; the launch traced here: 740 us
  waiting for transfers between devices  270 us (36%)
  local copies, waits for them, and re-layouts  241 us (32%)
  other arithmetic  115 us (15%)
  matrix products  77.5 us (10%)
  blocking collectives  22.5 us (3%)
  between operations  13.3 us (2%)
    gather x16, local copies, waits for them, and re-layouts, pair_products(): jnp.take(slot_cabs, slots.reshape(-1), axis=0)  125 us
    reduce_scatter x1, waiting for transfers between devices, sent_together(): lax.psum_scatter(both, axis, scatter_dimension=dim, tiled=True)  87.8 us
    gather x16, local copies, waits for them, and re-layouts, pair_products(): jnp.take(slot_pao, slots.reshape(-1), axis=0)  80.2 us
    all_gather x1, waiting for transfers between devices, shards(): lax.all_gather(cabs_blocks, 'atom', axis=0, tiled=True)  76.2 us
    all_gather x1, waiting for transfers between devices, shards(): lax.all_gather(pao_blocks, 'atom', axis=0, tiled=True)  63.6 us
    select_n x16, other arithmetic, pair_products(): jnp.take(slot_cabs, slots.reshape(-1), axis=0)  52.2 us
    dot_general x16, matrix products, pair_products(): jnp.einsum('pia,pja->pij', rows_pao, rows_cabs, preferred_element_type=jn...  43.9 us
    all_gather x1, waiting for transfers between devices, shards(): coupling_full = lax.all_gather(coupling_rows, 'aux', axis=1, tiled=True)  41 us
  transfers between devices with their start and end apart: 4, of which 4 were waited for; matrix products, arithmetic and copies ran while one was open for 2% of the time, Pallas kernels for 0%

commit v1 on v0

--- a/solution.py
+++ b/solution.py
@@ -2,6 +2,13 @@
 import jax.numpy as jnp
 from jax import lax
 from jax.sharding import PartitionSpec as P
+
+
+def swapped_in(block, mesh_axis, along):
+    size = lax.axis_size(mesh_axis)
+    shards = jnp.stack([block for _ in range(size)])
+    shards = lax.all_to_all(shards, mesh_axis, split_axis=0, concat_axis=0)
+    return jnp.concatenate(shards, axis=along)
 
 
 def sent_together(arrays, axis, dim, along):
@@ -36,7 +43,7 @@
     wanted = jnp.max(jnp.where(matches, flat_blocks[:, None], -1), axis=0)
     every_pao, every_cabs, every_weight = collect(
         (
-            lax.all_gather(pao_blocks, "atom", axis=0, tiled=True),
+            swapped_in(pao_blocks, "atom", 0),
             lax.all_gather(cabs_blocks, "atom", axis=0, tiled=True),
             lax.all_gather(cabs_weight, "atom", axis=0, tiled=True),
         )

time: 743 us -> 847 us (1.14)
  waiting for transfers between devices: 270 us -> 360 us
  starting transfers between devices: 0.12 us -> 9.86 us
    all_to_all x0 -> x1, waiting for transfers between devices: none -> 175 us  [swapped_in(): shards = lax.all_to_all(shards, mesh_axis, split_axis=0, concat_axis=0)]
    all_gather x1, waiting for transfers between devices: 76.2 us -> 11.3 us  [shards(): lax.all_gather(cabs_blocks, 'atom', axis=0, tiled=True)]
    all_gather x1 -> x0, waiting for transfers between devices: 63.6 us -> none  [shards(): lax.all_gather(pao_blocks, 'atom', axis=0, tiled=True)]
    reduce_scatter x1, waiting for transfers between devices: 87.8 us -> 131 us  [sent_together(): lax.psum_scatter(both, axis, scatter_dimension=dim, tiled=True)]
    all_to_all x0 -> x1, starting transfers between devices: none -> 9.77 us  [swapped_in(): shards = lax.all_to_all(shards, mesh_axis, split_axis=0, concat_axis=0)]
  transfers between devices with their start and end apart: 4 -> 4, of which waited for: 4 -> 4; matrix products, arithmetic and copies ran while one was open for 2% -> 3% of each run, Pallas kernels for 0% -> 0%
where the time goes in v1:
time: 847 us; the launch traced here: 845 us
  waiting for transfers between devices  360 us (43%)
  local copies, waits for them, and re-layouts  248 us (29%)
  other arithmetic  114 us (13%)
  matrix products  77.4 us (9%)
  blocking collectives  22.5 us (3%)
  between operations  13.3 us (2%)
  starting transfers between devices  9.86 us (1%)
    all_to_all x1, waiting for transfers between devices, swapped_in(): shards = lax.all_to_all(shards, mesh_axis, split_axis=0, concat_axis=0)  175 us
    reduce_scatter x1, waiting for transfers between devices, sent_together(): lax.psum_scatter(both, axis, scatter_dimension=dim, tiled=True)  131 us
    gather x16, local copies, waits for them, and re-layouts, pair_products(): jnp.take(slot_cabs, slots.reshape(-1), axis=0)  126 us
    gather x16, local copies, waits for them, and re-layouts, pair_products(): jnp.take(slot_pao, slots.reshape(-1), axis=0)  80.5 us
    select_n x16, other arithmetic, pair_products(): jnp.take(slot_cabs, slots.reshape(-1), axis=0)  52.2 us
    dot_general x16, matrix products, pair_products(): jnp.einsum('pia,pja->pij', rows_pao, rows_cabs, preferred_element_type=jn...  43.9 us
    all_gather x1, waiting for transfers between devices, shards(): coupling_full = lax.all_gather(coupling_rows, 'aux', axis=1, tiled=True)  41 us
    select_n x32, other arithmetic, pair_products(): jnp.take(slot_pao, slots.reshape(-1), axis=0)  34.6 us
  transfers between devices with their start and end apart: 4, of which 4 were waited for; matrix products, arithmetic and copies ran while one was open for 3% of the time, Pallas kernels for 0%

profile of v1, /device:TPU:1, one launch (start us, length us, event | category | flops | bytes accessed | tf_op | source)
XLA Modules:
  0.0 844.6 jit_solution(15673859555926879150)
XLA Ops:
  7.3 6.1 stack.2
  13.3 9.8 %all-to-all-start = ((bf16[32,2,24,3840]{3,2,1,0:T(8,128)(2,1)}), bf16[32,2,24,3840]{3,2,1,0:T(8,128)(2,1)}, u32[]{:S(2)}, u32[]{:S(2)}) async-start(bf16[32,2,24,3840]{3,2,1,0:T(8,128)(2,1)} %stack.2), calls=%async_computation | async-start | bytes 23592960 | tf_op jit(solution)/shard_map/all_to_all | solution.py:10
  23.8 175.5 %all-to-all-done = bf16[32,2,24,3840]{3,2,1,0:T(8,128)(2,1)} async-done(((bf16[32,2,24,3840]{3,2,1,0:T(8,128)(2,1)}), bf16[32,2,24,3840]{3,2,1,0:T(8,128)(2,1)}, u32[]{:S(2)}, u32[]{:S(2)}) %all-to-all-start) | async-done | bytes 11796512 | tf_op jit(solution)/shard_map/all_to_all | solution.py:10
  199.3 8.2 gather_fusion.2
  207.5 5.9 broadcast_select_fusion.1
  213.4 11.3 %all-gather.4.cloned.1.call-done = bf16[64,48,3840]{2,1,0:T(8,128)(2,1)} async-done(((bf16[2,48,3840]{2,1,0:T(8,128)(2,1)}), bf16[64,48,3840]{2,1,0:T(8,128)(2,1)}) %all-gather.4.cloned.1.call-update) | async-done | bytes 23592976 | tf_op jit(solution)/shard_map/all_gather | solution.py:47
  224.7 14.1 %gather_fusion.3 = bf16[32,48,3840]{2,1,0:T(8,128)(2,1)} fusion(bf16[64,48,3840]{2,1,0:T(8,128)(2,1)} %all-gather.4.cloned.1.call-done, s32[1024]{0:T(1024)S(1)} %pad_clamp_fusion.2), kind=kCustom, calls=%fused_computation.3 | custom fusion | bytes 23593088 | tf_op jit(solution)/shard_map/jit(_take)/gather | solution.py:53
  238.8 10.3 %broadcast_select_fusion = bf16[32,48,3840]{2,1,0:T(8,128)(2,1)} fusion(bf16[32,48,3840]{2,1,0:T(8,128)(2,1)} %gather_fusion.3, pred[32]{0:T(512)(128)(4,1)S(1)} %broadcast_compare_fusion), kind=kLoop, calls=%fused_computation.18 | loop fusion | flops 5898240 | bytes 23592992 | tf_op jit(solution)/shard_map/jit(_take)/select_n | solution.py:53
  249.1 369.4 %while.12 = (s32[]{:T(128)}, f32[16,4,96,96]{3,2,1,0:T(8,128)}, f32[16,4,96,192]{3,2,1,0:T(8,128)}, s32[16,4,4]{2,1,0:T(4,128)S(1)}, bf16[32,24,3840]{2,1,0:T(8,...) while((s32[]{:T(128)}, f32[16,4,96,96]{3,2,1,0:T(8,128)}, f32[16,4,96,192]{3,2,1,0:T(8,128)}, ...), condition=%wide.region_2.3_spmd, body=%wide.region_1.2_spmd.sunk | while | flops 853771392 | bytes 50735296 | solution.py:74
  249.2 5.0 gather_fusion
  256.6 7.8 gather_fusion.1
  264.6 3.3 bitcast_select_fusion.5
  272.3 5.0 gather_fusion
  279.7 7.8 gather_fusion.1
  287.7 3.3 bitcast_select_fusion.5
  295.4 5.0 gather_fusion
  302.8 7.8 gather_fusion.1
  310.8 3.3 bitcast_select_fusion.5
  318.5 5.0 gather_fusion
  325.9 7.8 gather_fusion.1
  333.9 3.3 bitcast_select_fusion.5
  341.6 5.0 gather_fusion
  349.0 7.8 gather_fusion.1
  357.0 3.3 bitcast_select_fusion.5
  364.7 5.0 gather_fusion
  372.1 7.8 gather_fusion.1
  380.1 3.3 bitcast_select_fusion.5
  387.8 5.0 gather_fusion
  395.2 7.8 gather_fusion.1
  403.2 3.3 bitcast_select_fusion.5
  406.4 2.8 fusion.36
  410.9 5.0 gather_fusion
  418.3 7.8 gather_fusion.1
  426.3 3.3 bitcast_select_fusion.5
  434.0 5.0 gather_fusion
  441.3 7.8 gather_fusion.1
  449.3 3.3 bitcast_select_fusion.5
  457.1 5.0 gather_fusion
  464.4 7.8 gather_fusion.1
  472.4 3.3 bitcast_select_fusion.5
  480.1 5.0 gather_fusion
  487.5 7.8 gather_fusion.1
  495.5 3.3 bitcast_select_fusion.5
  503.2 5.0 gather_fusion
  510.6 7.8 gather_fusion.1
  518.6 3.3 bitcast_select_fusion.5
  526.3 5.0 gather_fusion
  533.7 7.8 gather_fusion.1
  541.7 3.3 bitcast_select_fusion.5
  549.4 5.0 gather_fusion
  556.7 7.8 gather_fusion.1
  564.7 3.3 bitcast_select_fusion.5
  572.4 5.0 gather_fusion
  579.8 7.8 gather_fusion.1
  587.8 3.3 bitcast_select_fusion.5
  595.5 5.0 gather_fusion
  602.9 7.8 gather_fusion.1
  610.9 3.3 bitcast_select_fusion.5
  623.6 6.1 pad_maximum_fusion
  629.9 131.3 %reduce-scatter.2.cloned.1.call-done = f32[64,24,288]{2,1,0:T(8,128)} async-done(((f32[64,96,288]{2,1,0:T(8,128)}), f32[64,24,288]{2,1,0:T(8,128)}) %reduce-scatter.2.cloned.1.call-update) | async-done | bytes 1769488 | tf_op jit(solution)/shard_map/reduce_scatter | solution.py:21
  761.2 3.4 split.9
  764.8 22.5 %all-gather = bf16[32,2,48]{2,1,0:T(2,128)(2,1)S(1)} all-gather(bf16[1,2,48]{2,1,0:T(2,128)(2,1)S(1)} %bitcast.65), channel_id=1, replica_groups=mesh['atom'=32,'aux'=4] {'atom'}, dimensions={0}, use_global_device_ids=true | all-gather | bytes 6336 | tf_op jit(solution)/shard_map/all_gather | solution.py:48
  789.1 41.0 %all-gather.6.cloned.1.call-done = f32[64,96,192]{2,1,0:T(8,128)} async-done(((f32[64,24,192]{2,1,0:T(8,128)}), f32[64,96,192]{2,1,0:T(8,128)}) %all-gather.6.cloned.1.call-update) | async-done | bytes 4718608 | tf_op jit(solution)/shard_map/all_gather | solution.py:91
  830.0 8.0 fusion.7
  (218 shorter events, 116.4 us)
Async XLA Ops:
  6.5 218.2 %all-gather.4.cloned.1.call-start = ((), (), s32[]{:S(2)}) async-start(), calls=%async_computation.2 | async-start | bytes 24330240 | tf_op jit(solution)/shard_map/all_gather | solution.py:47
  13.3 9.9 %copy-start.2 = (s32[64,4]{0,1:T(4,128)S(1)}, s32[64,4]{0,1:T(4,128)}, u32[]{:S(2)}) copy-start(s32[64,4]{0,1:T(4,128)} %param.11) | copy-start | bytes 3076
  13.3 10.2 %copy-start.3 = (s32[64]{0:T(128)S(1)}, s32[64]{0:T(128)}, u32[]{:S(2)}) copy-start(s32[64]{0:T(128)} %param.12) | copy-start | bytes 772
  13.3 10.4 %copy-start.4 = (s32[64]{0:T(128)S(1)}, s32[64]{0:T(128)}, u32[]{:S(2)}) copy-start(s32[64]{0:T(128)} %param.13) | copy-start | bytes 772
  13.3 185.9 %all-to-all-start = ((bf16[32,2,24,3840]{3,2,1,0:T(8,128)(2,1)}), bf16[32,2,24,3840]{3,2,1,0:T(8,128)(2,1)}, u32[]{:S(2)}, u32[]{:S(2)}) async-start(bf16[32,2,24,3840]{3,2,1,0:T(8,128)(2,1)} %stack.2), calls=%async_computation | async-start | bytes 23592960 | tf_op jit(solution)/shard_map/all_to_all | solution.py:10
  23.1 738.1 %reduce-scatter.2.cloned.1.call-start = ((), (), s32[]{:S(2)}) async-start(), calls=%async_computation.3 | async-start | bytes 11796480 | tf_op jit(solution)/shard_map/reduce_scatter | solution.py:21
  618.5 3.7 copy-start
  629.8 135.0 %copy-start.5 = (bf16[2,48]{1,0:T(2,128)(2,1)S(1)}, bf16[2,48]{1,0:T(2,128)(2,1)}, u32[]{:S(2)}) copy-start(bf16[2,48]{1,0:T(2,128)(2,1)} %param.10) | copy-start | bytes 580
  629.8 200.2 %all-gather.6.cloned.1.call-start = ((), (), s32[]{:S(2)}) async-start(), calls=%async_computation.4 | async-start | bytes 7864320 | tf_op jit(solution)/shard_map/all_gather | solution.py:91
  761.2 68.9 %copy-start.1 = (f32[64,24,288]{2,1,0:T(8,128)S(1)}, f32[64,24,288]{2,1,0:T(8,128)}, u32[]{:S(2)}) copy-start(f32[64,24,288]{2,1,0:T(8,128)} %reduce-scatter.2.cloned.1.call-done) | copy-start | bytes 5308420
Sparse Core Ops, SparseCore 0:
  9.6 215.0 all-gather.3
  629.9 131.2 reduce-scatter.1
  764.8 65.2 all-gather.5
